TPU v7x, 256 devices: a whole 4x4x8 slice. The times are simulated.
256 devices in a mesh: batch: 32 (over x, z_hi, core), hidden: 8 (over z_lo, y).
Axes of the slice: x: 4, y: 4, z: 8 (z_hi: 4, z_lo: 2; z = z_hi * 2 + z_lo), core: 2. Of those that a mesh axis runs over, the one named last changes fastest.
Arguments:
- features: bfloat16 [12288, 512], P('batch'), may hold values from -6 to 6
- w_first: bfloat16 [512, 8192], P('batch', 'hidden'), may hold values from -0.25 to 0.25
- w_second: bfloat16 [8192, 4096], P('hidden', 'batch'), may hold values from -0.0625 to 0.0625
- w_head: bfloat16 [4096, 8], P('hidden'), may hold values from -0.09375 to 0.09375
- rewards: float32 [8, 12288], P(None, 'batch'), may hold values from -1.75 to 1.75
- discount: float32 [8], replicated, as said below
- trace: float32 [8], replicated, as said below
- episode: int32 [12288], P('batch'), may hold values from 0 to 32, as said below
Outputs:
- advantages: float32 [8, 12288], P(None, 'batch')
- loss: float32 [], replicated
- grad_first: float32 [512, 8192], P('batch', 'hidden')
- grad_second: float32 [8192, 4096], P('hidden', 'batch')
- grad_head: float32 [4096, 8], P('hidden')
Inputs may be any that keep to these rules, and one draw needn't show every extreme that they name: Each discount lies between 0.875 and 1. Each trace factor lies between 0.875 and 1. episode numbers never fall along the rollout and rise by one at each episode start; each block of 384 timesteps of one index of batch holds exactly one episode start besides the rollout's own start at timestep 0, and that start never falls on the block's first timestep; the rollout begins with episode 0.
All inputs are finite; a program needn't handle non-finite values.
Results may differ from a plain program's by a relative error of at most 0.018.
Values may be sent and summed in bfloat16 or wider, within the bound.
A program may use at most 128 MiB of HBM per device.

v0:
```python
import jax
import jax.numpy as jnp
from jax import lax
from jax.sharding import PartitionSpec as P


def sent_to_all(array, axis):
    length = lax.axis_size(axis)
    return lax.all_to_all(
        jnp.broadcast_to(array[None], (length, *array.shape)), axis, 0, 0, tiled=True
    )


def over_copies(array, axis):
    return sent_to_all(array, axis).sum(axis=0)


def passed_along(value, axis, steps):
    count = lax.axis_size(axis)
    initial, last = (max(0, -steps), min(count, count - steps))
    return lax.ppermute(value, axis, [(source, source + steps) for source in range(initial, last)])


def collected_together(array, axis):
    leaves = jax.tree.leaves(array)
    turns = sorted(range(len(leaves)), key=lambda k: -leaves[k].size)
    width = (1, *leaves[turns[0]].shape)[-1]
    lines = [
        jnp.pad(leaves[k].reshape(-1), (0, -leaves[k].size % width)).reshape(-1, width)
        for k in turns
    ]
    both, at, found = (sent_to_all(jnp.concatenate(lines), axis), 0, {})
    for k, line in zip(turns, lines):
        share = both[:, at : at + len(line)].reshape(len(both), -1)
        found[k] = share[:, : leaves[k].size].reshape(-1, *leaves[k].shape)
        at += len(line)
    numbers = iter(range(len(leaves)))
    return jax.tree.map(lambda _: found[next(numbers)], array)


def joined_by_halves(pieces, combine):
    while len(jax.tree.leaves(pieces)[0]) > 1:
        pieces = jax.vmap(combine)(
            *(jax.tree.map(lambda part: part[side::2], pieces) for side in (0, 1))
        )
    return jax.tree.map(lambda part: part[0], pieces)


def prefix(array, axis, combine, identity):
    length, position = (lax.axis_size(axis), lax.axis_index(axis))
    passed = jnp.arange(length) > position

    def kept(part, zero, own):
        part = jnp.where(
            passed.reshape(-1, *(1 for _ in own.shape)), part, jnp.asarray(zero, own.dtype)
        )
        return part[::-1]

    pieces = collected_together(array, axis)
    return joined_by_halves(jax.tree.map(kept, pieces, identity, array), combine)


def cut_along(array, dim, length):
    before, after = (array.shape[:dim], array.shape[dim + 1 :])
    return jnp.moveaxis(array.reshape(*before, length, -1, *after), dim, 0)


def summed_on_arrival(array, axis, dim):
    length = lax.axis_size(axis)
    pieces = lax.all_to_all(cut_along(array, dim, length), axis, 0, 0, tiled=True)
    return jnp.sum(pieces.astype(jnp.float32), axis=0)


def chain_maps(farther, nearer):
    return (farther[0] * nearer[0], nearer[1] + nearer[0] * farther[1])


def silu_slope(value):
    sigmoid_value = jax.nn.sigmoid(value)
    return sigmoid_value * (1.0 + value * (1.0 - sigmoid_value))


def contract(left, right, left_dim, right_dim):
    return lax.dot_general(
        left, right, (((left_dim,), (right_dim,)), ((), ())), preferred_element_type=jnp.float32
    )


def shards(features, w_first, w_second, w_head, rewards, discount, trace, episode):
    rows_here = features.shape[0]
    heads = w_head.shape[1]
    columns = features
    pre_first = jnp.dot(
        columns,
        lax.all_gather(w_first, "batch", axis=0, tiled=True),
        preferred_element_type=jnp.float32,
    )
    hidden_first = jax.nn.silu(pre_first).astype(jnp.bfloat16)
    partial_value = jnp.dot(
        hidden_first,
        lax.all_gather(w_second, "batch", axis=1, tiled=True),
        preferred_element_type=jnp.float32,
    )
    pre_second = lax.psum_scatter(
        partial_value.astype(jnp.bfloat16), "hidden", scatter_dimension=1, tiled=True
    ).astype(jnp.float32)
    hidden_second = jax.nn.silu(pre_second).astype(jnp.bfloat16)
    values = over_copies(
        jnp.dot(hidden_second, w_head, preferred_element_type=jnp.float32), "hidden"
    )
    values_t = values.T
    next_value = passed_along(values_t[:, :1], "batch", -1)
    next_first = passed_along(episode[:1] + 1, "batch", -1)
    following = jnp.concatenate([episode[1:] + 1, next_first])
    keep = (following == episode + 1).astype(jnp.float32)
    value_after = jnp.concatenate([values_t[:, 1:], next_value], axis=1)
    delta = rewards + discount[:, None] * keep[None, :] * value_after - values_t
    factor = discount[:, None] * trace[:, None] * keep[None, :]
    reach, local_adv = lax.associative_scan(chain_maps, (factor, delta), reverse=True, axis=1)
    identity = (jnp.ones((heads,), jnp.float32), jnp.zeros((heads,), jnp.float32))
    _, entering = prefix((reach[:, 0], local_adv[:, 0]), "batch", chain_maps, identity)
    advantages = local_adv + reach * entering[:, None]
    slope_value = (-advantages.T).astype(jnp.bfloat16)
    slope_share = (contract(slope_value, w_head, 1, 1) * silu_slope(pre_second)).astype(
        jnp.bfloat16
    )
    slope_second = lax.all_gather(slope_share, "hidden", axis=1, tiled=True)
    head_term = contract(hidden_second, slope_value, 0, 0)
    grad_head, loss_sum = (
        over_copies(head_term, "batch"),
        over_copies(jnp.sum(advantages * advantages), "batch"),
    )
    loss = 0.5 * loss_sum / (rows_here * lax.axis_size("batch") * heads)
    columns = slope_second
    back_first = contract(columns, lax.all_gather(w_second, "batch", axis=1, tiled=True), 1, 1)
    slope_first = (back_first * silu_slope(pre_first)).astype(jnp.bfloat16)
    columns = slope_second
    grad_second = (
        lax.psum_scatter(
            contract(columns, hidden_first, 0, 0).astype(jnp.bfloat16),
            "batch",
            scatter_dimension=0,
            tiled=True,
        )
        .astype(jnp.float32)
        .T
    )
    columns = features
    grad_first = summed_on_arrival(
        contract(columns, slope_first, 0, 0).astype(jnp.bfloat16), "batch", 0
    )
    return (advantages, loss, grad_first, grad_second, grad_head)


def solution(mesh):
    placed = (
        P("batch", None),
        P("batch", "hidden"),
        P("hidden", "batch"),
        P("hidden", None),
        P(None, "batch"),
        P(),
        P(),
        P("batch"),
    )
    return jax.shard_map(
        shards,
        mesh=mesh,
        in_specs=placed,
        out_specs=(
            P(None, "batch"),
            P(),
            P("batch", "hidden"),
            P("hidden", "batch"),
            P("hidden", None),
        ),
        check_vma=False,
    )
```

profile of v0, /device:TPU:8, one launch (start us, length us, event | category | flops | bytes accessed | tf_op | source)
XLA Modules:
  0.0 450.4 jit_solution(7222530237722029714)
XLA Ops:
  7.2 0.7 all-gather.4.cloned.1.call-update
  8.0 0.7 all-gather.6.cloned.1.call-update
  8.7 56.7 %all-gather.4.cloned.1.call-done = bf16[512,1024]{1,0:T(8,128)(2,1)} async-done(((bf16[16,1024]{1,0:T(8,128)(2,1)}), bf16[512,1024]{1,0:T(8,128)(2,1)}) %all-gather.4.cloned.1.call-update) | async-done | bytes 1048592 | tf_op jit(solution)/shard_map/all_gather | solution.py:95
  65.5 1.8 fusion.20
  67.3 82.4 %all-gather.6.cloned.1.call-done = bf16[1024,4096]{1,0:T(8,128)(2,1)} async-done(((bf16[1024,128]{1,0:T(8,128)(2,1)}), bf16[1024,4096]{1,0:T(8,128)(2,1)}) %all-gather.6.cloned.1.call-update) | async-done | bytes 8388624 | tf_op jit(solution)/shard_map/all_gather | solution.py:101
  149.7 8.2 %convolution_convert_fusion.1 = bf16[384,4096]{1,0:T(8,128)(2,1)} fusion(bf16[1024,4096]{1,0:T(8,128)(2,1)} %all-gather.6.cloned.1.call-done, f32[384,1024]{1,0:T(8,128)S(1)} %fusion.20), kind=kOutput, calls=%fused_computation.1 | convolution fusion | flops 3224764416 | bytes 13107200 | tf_op jit(solution)/shard_map/dot_general | solution.py:99
  157.9 0.6 copy-done.5
  158.6 0.5 slice.355
  159.7 1.3 collective-permute-start
  161.1 43.1 %reduce-scatter.3.cloned.1.call-done = bf16[384,512]{1,0:T(8,128)(2,1)} async-done(((bf16[384,4096]{1,0:T(8,128)(2,1)}), bf16[384,512]{1,0:T(8,128)(2,1)}) %reduce-scatter.3.cloned.1.call-update) | async-done | bytes 393232 | tf_op jit(solution)/shard_map/reduce_scatter | solution.py:104
  204.3 1.2 fusion.4
  205.5 0.2 fusion.21
  205.7 0.7 broadcast_in_dim.26
  206.4 5.4 %all-to-all-start = ((f32[8,384,8]{1,2,0:T(8,128)}), f32[8,384,8]{1,2,0:T(8,128)S(1)}, u32[]{:S(2)}, u32[]{:S(2)}) async-start(f32[8,384,8]{1,2,0:T(8,128)} %broadcast_in_dim.26), calls=%async_computation.1 | async-start | bytes 196608 | tf_op jit(solution)/shard_map/all_to_all | solution.py:9
  211.8 0.6 fusion.12
  212.4 4.4 all-to-all-done
  216.9 1.3 collective-permute-start.1
  218.2 1.8 collective-permute-done.1
  220.1 0.3 slice.371
  220.4 0.3 slice.365
  220.6 0.3 slice.361
  220.9 0.2 reverse.19
  221.3 0.2 slice.379
  221.5 0.2 slice.375
  221.6 0.2 slice.373
  221.9 0.3 slice.367
  222.2 0.3 slice.363
  222.4 0.3 slice.359
  222.7 0.2 reverse.18
  223.1 0.2 slice.376
  223.3 0.2 slice.374
  226.3 0.2 slice.370
  226.5 0.2 reverse.15
  230.4 0.2 pad.126
  230.9 0.3 pad.113
  231.3 0.3 pad.128
  231.7 0.3 pad.112
  232.0 0.3 pad.129
  232.3 0.2 add_reduce_fusion
  232.4 0.2 add_reduce_fusion.1
  232.6 0.6 broadcast_in_dim.28
  233.3 9.6 %all-to-all-start.1 = ((f32[32,2,8]{2,1,0:T(2,128)}), f32[32,2,8]{2,1,0:T(2,128)S(1)}, u32[]{:S(2)}, u32[]{:S(2)}) async-start(f32[32,2,8]{2,1,0:T(2,128)} %broadcast_in_dim.28), calls=%async_computation.2 | async-start | bytes 65536 | tf_op jit(solution)/shard_map/all_to_all | solution.py:9
  242.9 0.2 rev.4
  243.2 0.2 rev.5
  243.4 9.3 %all-to-all-done.1 = f32[32,2,8]{2,1,0:T(2,128)S(1)} async-done(((f32[32,2,8]{2,1,0:T(2,128)}), f32[32,2,8]{2,1,0:T(2,128)S(1)}, u32[]{:S(2)}, u32[]{:S(2)}) %all-to-all-start.1) | async-done | bytes 2080 | tf_op jit(solution)/shard_map/all_to_all | solution.py:9
  253.2 0.7 multiply_reduce_fusion
  253.9 1.2 fusion
  255.1 39.2 %all-gather.8.cloned.1.call-done = bf16[384,4096]{1,0:T(8,128)(2,1)} async-done(((bf16[384,512]{1,0:T(8,128)(2,1)}), bf16[384,4096]{1,0:T(8,128)(2,1)}) %all-gather.8.cloned.1.call-update) | async-done | bytes 3145744 | tf_op jit(solution)/shard_map/all_gather | solution.py:127
  294.4 8.8 %convolution_convert_fusion = bf16[4096,1024]{1,0:T(8,128)(2,1)} fusion(bf16[384,4096]{1,0:T(8,128)(2,1)} %all-gather.8.cloned.1.call-done, f32[384,1024]{1,0:T(8,128)S(1)} %fusion.20), kind=kOutput, calls=%fused_computation | convolution fusion | flops 3227385856 | bytes 13107200 | tf_op jit(solution)/shard_map/dot_general | solution.py:84
  303.2 1.3 broadcast_in_dim.52
  304.5 9.1 %all-to-all-start.2 = ((f32[32,1,1]{2,1,0:T(1,128)}), f32[32,1,1]{2,1,0:T(1,128)S(1)}, u32[]{:S(2)}, u32[]{:S(2)}) async-start(f32[32,1,1]{2,1,0:T(1,128)} %broadcast_in_dim.52), calls=%async_computation.3 | async-start | bytes 32768 | tf_op jit(solution)/shard_map/all_to_all | solution.py:9
  313.8 9.6 %all-to-all-done.2 = f32[32,1,1]{2,1,0:T(1,128)S(1)} async-done(((f32[32,1,1]{2,1,0:T(1,128)}), f32[32,1,1]{2,1,0:T(1,128)S(1)}, u32[]{:S(2)}, u32[]{:S(2)}) %all-to-all-start.2) | async-done | bytes 160 | tf_op jit(solution)/shard_map/all_to_all | solution.py:9
  323.3 0.9 broadcast_in_dim.53
  324.2 3.9 all-to-all-start.4
  328.1 10.0 %convolution_convert_fusion.2 = bf16[1024,512]{0,1:T(8,128)(2,1)} fusion(bf16[384,512]{1,0:T(8,128)(2,1)S(1)} %copy-done, f32[384,1024]{1,0:T(8,128)S(1)} %fusion.20, bf16[384,4096]{1,0:T(8,128)(2,1)} %all-gather.8.cloned.1.call-done, bf16[1024,4096]{1,0:T(8,128)(2,1)} %all-gather.6.cloned.1.call-done), kind=kOutput, calls=%fused_computation.6 | convolution fusion | flops 3627941888 | bytes 14548992 | tf_op jit(solution)/shard_map/dot_general | solution.py:84
  338.1 8.0 %all-to-all-done.4 = f32[32,512,8]{1,2,0:T(8,128)S(1)} async-done(((f32[32,512,8]{1,2,0:T(8,128)}), f32[32,512,8]{1,2,0:T(8,128)S(1)}, u32[]{:S(2)}, u32[]{:S(2)}) %all-to-all-start.4) | async-done | bytes 524320 | tf_op jit(solution)/shard_map/all_to_all | solution.py:9
  346.1 4.3 all-to-all-start.3
  350.5 0.6 reduce_sum.47
  351.8 0.7 reduce_sum.49
  352.4 28.6 %all-to-all-done.3 = bf16[32,16,1024]{2,1,0:T(8,128)(2,1)S(1)} async-done(((bf16[32,16,1024]{2,1,0:T(8,128)(2,1)}), bf16[32,16,1024]{2,1,0:T(8,128)(2,1)S(1)}, u32[]{:S(2)}, u32[]{:S(2)}) %all-to-all-start.3) | async-done | bytes 1048608 | tf_op jit(solution)/shard_map/all_to_all | solution.py:70
  381.0 0.8 convert_reduce_fusion
  381.8 59.0 %reduce-scatter.5.cloned.1.call-done = bf16[128,1024]{1,0:T(8,128)(2,1)} async-done(((bf16[4096,1024]{1,0:T(8,128)(2,1)}), bf16[128,1024]{1,0:T(8,128)(2,1)}) %reduce-scatter.5.cloned.1.call-update) | async-done | bytes 262160 | tf_op jit(solution)/shard_map/reduce_scatter | solution.py:139
  440.7 1.0 convert_bitcast_fusion
  441.7 1.0 copy.22
  (170 shorter events, 8.6 us)
Async XLA Ops:
  7.2 58.3 %copy-start = (bf16[384,512]{1,0:T(8,128)(2,1)S(1)}, bf16[384,512]{1,0:T(8,128)(2,1)}, u32[]{:S(2)}) copy-start(bf16[384,512]{1,0:T(8,128)(2,1)} %param.8) | copy-start | bytes 1179652
  7.2 58.3 %all-gather.4.cloned.1.call-start = ((), (), s32[]{:S(2)}) async-start(), calls=%async_computation.7 | async-start | bytes 1081344 | tf_op jit(solution)/shard_map/all_gather | solution.py:95
  7.9 141.8 %all-gather.6.cloned.1.call-start = ((), (), s32[]{:S(2)}) async-start(), calls=%async_computation.8 | async-start | bytes 8650752 | tf_op jit(solution)/shard_map/all_gather | solution.py:101
  8.7 195.6 %reduce-scatter.3.cloned.1.call-start = ((), (), s32[]{:S(2)}) async-start(), calls=%async_computation.9 | async-start | bytes 3538944 | tf_op jit(solution)/shard_map/reduce_scatter | solution.py:104
  157.9 0.7 copy-start.5
  157.9 3.2 copy-start.6
  157.9 3.2 copy-start.7
  157.9 47.6 %copy-start.4 = (bf16[512,8]{0,1:T(8,128)(2,1)S(1)}, bf16[512,8]{0,1:T(8,128)(2,1)}, u32[]{:S(2)}) copy-start(bf16[512,8]{0,1:T(8,128)(2,1)} %param.11) | copy-start | bytes 24580
  158.5 61.4 %copy-start.3 = (f32[8,384]{1,0:T(8,128)S(1)}, f32[8,384]{1,0:T(8,128)}, u32[]{:S(2)}) copy-start(f32[8,384]{1,0:T(8,128)} %param.12) | copy-start | bytes 36868
  159.7 52.1 %collective-permute-start = (s32[1]{0:T(128)}, s32[1]{0:T(128)}, u32[]{:S(2)}, u32[]{:S(2)}) collective-permute-start(s32[1]{0:T(128)} %add.218), channel_id=1, source_target_pairs={{8,0},{16,8},{24,16},{32,24},{40,32},{48,40},{56,48},{64,56},{72,6... | collective-permute-start | bytes 20 | tf_op jit(solution)/shard_map/ppermute | solution.py:21
  205.7 48.1 %copy-start.1 = (bf16[384,512]{1,0:T(8,128)(2,1)S(1)}, bf16[384,512]{1,0:T(8,128)(2,1)}, u32[]{:S(2)}) copy-start(bf16[384,512]{1,0:T(8,128)(2,1)} %reduce-scatter.3.cloned.1.call-done) | copy-start | bytes 1179652
  206.4 10.4 %all-to-all-start = ((f32[8,384,8]{1,2,0:T(8,128)}), f32[8,384,8]{1,2,0:T(8,128)S(1)}, u32[]{:S(2)}, u32[]{:S(2)}) async-start(f32[8,384,8]{1,2,0:T(8,128)} %broadcast_in_dim.26), calls=%async_computation.1 | async-start | bytes 196608 | tf_op jit(solution)/shard_map/all_to_all | solution.py:9
  216.9 3.1 collective-permute-start.1
  233.3 19.4 %all-to-all-start.1 = ((f32[32,2,8]{2,1,0:T(2,128)}), f32[32,2,8]{2,1,0:T(2,128)S(1)}, u32[]{:S(2)}, u32[]{:S(2)}) async-start(f32[32,2,8]{2,1,0:T(2,128)} %broadcast_in_dim.28), calls=%async_computation.2 | async-start | bytes 65536 | tf_op jit(solution)/shard_map/all_to_all | solution.py:9
  242.9 51.5 %all-gather.8.cloned.1.call-start = ((), (), s32[]{:S(2)}) async-start(), calls=%async_computation.10 | async-start | bytes 3538944 | tf_op jit(solution)/shard_map/all_gather | solution.py:127
  253.9 59.8 %copy-start.2 = (f32[8,384]{1,0:T(8,128)}, f32[8,384]{1,0:T(8,128)S(1)}, u32[]{:S(2)}) copy-start(f32[8,384]{1,0:T(8,128)S(1)} %get-tuple-element.26) | copy-start | bytes 36868
  255.1 185.7 %reduce-scatter.5.cloned.1.call-start = ((), (), s32[]{:S(2)}) async-start(), calls=%async_computation.11 | async-start | bytes 8650752 | tf_op jit(solution)/shard_map/reduce_scatter | solution.py:139
  304.5 18.8 %all-to-all-start.2 = ((f32[32,1,1]{2,1,0:T(1,128)}), f32[32,1,1]{2,1,0:T(1,128)S(1)}, u32[]{:S(2)}, u32[]{:S(2)}) async-start(f32[32,1,1]{2,1,0:T(1,128)} %broadcast_in_dim.52), calls=%async_computation.3 | async-start | bytes 32768 | tf_op jit(solution)/shard_map/all_to_all | solution.py:9
  324.2 22.0 %all-to-all-start.4 = ((f32[32,512,8]{1,2,0:T(8,128)}), f32[32,512,8]{1,2,0:T(8,128)S(1)}, u32[]{:S(2)}, u32[]{:S(2)}) async-start(f32[32,512,8]{1,2,0:T(8,128)} %broadcast_in_dim.53), calls=%async_computation.6 | async-start | bytes 1048576 | tf_op jit(solution)/shard_map/all_to_all | solution.py:9
  346.1 34.9 %all-to-all-start.3 = ((bf16[32,16,1024]{2,1,0:T(8,128)(2,1)}), bf16[32,16,1024]{2,1,0:T(8,128)(2,1)S(1)}, u32[]{:S(2)}, u32[]{:S(2)}) async-start(bf16[32,16,1024]{2,1,0:T(8,128)(2,1)} %bitcast.42), calls=%async_computation.4 | async-start | bytes 2097152 | tf_op jit(solution)/shard_map/all_to_all | solution.py:70
Sparse Core Ops, SparseCore 0:
  10.5 54.8 all-gather.3
  67.9 81.7 all-gather.5
  158.0 46.1 reduce-scatter.2
  255.2 39.1 all-gather.7
  303.3 137.3 reduce-scatter.4
where the time goes:
time: 451 us; the launch traced here: 450 us
  waiting for transfers between devices  343 us (76%)
  starting transfers between devices  35.1 us (8%)
  matrix products  30.4 us (7%)
  between operations  16.8 us (4%)
  local copies, waits for them, and re-layouts  16.5 us (4%)
  other arithmetic  8.07 us (2%)
    all_gather x1, waiting for transfers between devices, shards(): lax.all_gather(w_second, 'batch', axis=1, tiled=True)  82.4 us
    reduce_scatter x1, waiting for transfers between devices, shards(): lax.psum_scatter(contract(columns, hidden_first, 0, 0).astype(jnp.bfloat1...  59 us
    all_gather x1, waiting for transfers between devices, shards(): lax.all_gather(w_first, 'batch', axis=0, tiled=True)  56.7 us
    reduce_scatter x1, waiting for transfers between devices, shards(): lax.psum_scatter(partial_value.astype(jnp.bfloat16), 'hidden', scatter_di...  43.1 us
    all_gather x1, waiting for transfers between devices, shards(): slope_second = lax.all_gather(slope_share, 'hidden', axis=1, tiled=True)  39.2 us
    all_to_all x4, waiting for transfers between devices, sent_to_all(): lax.all_to_all(jnp.broadcast_to(array[None], (length, *array.shape)), axi...  31.2 us
    all_to_all x1, waiting for transfers between devices, summed_on_arrival(): lax.all_to_all(cut_along(array, dim, length), axis, 0, 0, tiled=True)  28.6 us
    all_to_all x4, starting transfers between devices, sent_to_all(): lax.all_to_all(jnp.broadcast_to(array[None], (length, *array.shape)), axi...  28 us
  transfers between devices with their start and end apart: 12, of which 11 were waited for; matrix products, arithmetic and copies ran while one was open for 4% of the time, Pallas kernels for 0%

commit v1 on v0

--- a/solution.py
+++ b/solution.py
@@ -124,7 +124,9 @@
     slope_share = (contract(slope_value, w_head, 1, 1) * silu_slope(pre_second)).astype(
         jnp.bfloat16
     )
-    slope_second = lax.all_gather(slope_share, "hidden", axis=1, tiled=True)
+    slope_second = jnp.concatenate(
+        lax.all_to_all(jnp.stack([slope_share] * lax.axis_size("hidden")), "hidden", 0, 0), axis=1
+    )
     head_term = contract(hidden_second, slope_value, 0, 0)
     grad_head, loss_sum = (
         over_copies(head_term, "batch"),

time: 451 us -> 446 us (0.989)
  blocking collectives: 0 us -> 40.8 us
  waiting for transfers between devices: 343 us -> 304 us
  starting transfers between devices: 35.1 us -> 29.4 us
    all_to_all x0 -> x1, blocking collectives: none -> 40.8 us  [shards(): lax.all_to_all(jnp.stack([slope_share] * lax.axis_size('hidden')), 'hidde...]
    all_gather x1 -> x0, waiting for transfers between devices: 39.2 us -> none  [shards(): slope_second = lax.all_gather(slope_share, 'hidden', axis=1, tiled=True)]
    all_to_all x4, starting transfers between devices: 28 us -> 22.7 us  [sent_to_all(): lax.all_to_all(jnp.broadcast_to(array[None], (length, *array.shape)), axi...]
  transfers between devices with their start and end apart: 12 -> 11, of which waited for: 11 -> 10; matrix products, arithmetic and copies ran while one was open for 4% -> 5% of each run, Pallas kernels for 0% -> 0%
where the time goes in v1:
time: 446 us; the launch traced here: 445 us
  waiting for transfers between devices  304 us (68%)
  blocking collectives  40.8 us (9%)
  starting transfers between devices  29.4 us (7%)
  matrix products  27.8 us (6%)
  local copies, waits for them, and re-layouts  18.6 us (4%)
  between operations  16.8 us (4%)
  other arithmetic  8.08 us (2%)
    all_gather x1, waiting for transfers between devices, shards(): lax.all_gather(w_second, 'batch', axis=1, tiled=True)  82.4 us
    reduce_scatter x1, waiting for transfers between devices, shards(): lax.psum_scatter(contract(columns, hidden_first, 0, 0).astype(jnp.bfloat1...  57.8 us
    all_gather x1, waiting for transfers between devices, shards(): lax.all_gather(w_first, 'batch', axis=0, tiled=True)  56.7 us
    reduce_scatter x1, waiting for transfers between devices, shards(): lax.psum_scatter(partial_value.astype(jnp.bfloat16), 'hidden', scatter_di...  43.1 us
    all_to_all x1, blocking collectives, shards(): lax.all_to_all(jnp.stack([slope_share] * lax.axis_size('hidden')), 'hidde...  40.8 us
    all_to_all x4, waiting for transfers between devices, sent_to_all(): lax.all_to_all(jnp.broadcast_to(array[None], (length, *array.shape)), axi...  31.4 us
    all_to_all x1, waiting for transfers between devices, summed_on_arrival(): lax.all_to_all(cut_along(array, dim, length), axis, 0, 0, tiled=True)  29.1 us
    all_to_all x4, starting transfers between devices, sent_to_all(): lax.all_to_all(jnp.broadcast_to(array[None], (length, *array.shape)), axi...  22.7 us
  transfers between devices with their start and end apart: 11, of which 10 were waited for; matrix products, arithmetic and copies ran while one was open for 5% of the time, Pallas kernels for 0%

profile of v1, /device:TPU:8, one launch (start us, length us, event | category | flops | bytes accessed | tf_op | source)
XLA Modules:
  0.0 445.4 jit_solution(14820151505460503589)
XLA Ops:
  7.2 0.7 all-gather.3.cloned.1.call-update
  8.0 0.7 all-gather.5.cloned.1.call-update
  8.7 56.7 %all-gather.3.cloned.1.call-done = bf16[512,1024]{1,0:T(8,128)(2,1)} async-done(((bf16[16,1024]{1,0:T(8,128)(2,1)}), bf16[512,1024]{1,0:T(8,128)(2,1)}) %all-gather.3.cloned.1.call-update) | async-done | bytes 1048592 | tf_op jit(solution)/shard_map/all_gather | solution.py:95
  65.5 1.8 fusion.20
  67.3 82.4 %all-gather.5.cloned.1.call-done = bf16[1024,4096]{1,0:T(8,128)(2,1)} async-done(((bf16[1024,128]{1,0:T(8,128)(2,1)}), bf16[1024,4096]{1,0:T(8,128)(2,1)}) %all-gather.5.cloned.1.call-update) | async-done | bytes 8388624 | tf_op jit(solution)/shard_map/all_gather | solution.py:101
  149.7 8.2 %convolution_convert_fusion.1 = bf16[384,4096]{1,0:T(8,128)(2,1)} fusion(bf16[1024,4096]{1,0:T(8,128)(2,1)} %all-gather.5.cloned.1.call-done, f32[384,1024]{1,0:T(8,128)S(1)} %fusion.20), kind=kOutput, calls=%fused_computation.1 | convolution fusion | flops 3224764416 | bytes 13107200 | tf_op jit(solution)/shard_map/dot_general | solution.py:99
  157.9 0.6 copy-done.6
  158.5 0.5 slice.355
  159.7 1.3 collective-permute-start
  161.1 43.1 %reduce-scatter.3.cloned.1.call-done = bf16[384,512]{1,0:T(8,128)(2,1)} async-done(((bf16[384,4096]{1,0:T(8,128)(2,1)}), bf16[384,512]{1,0:T(8,128)(2,1)}) %reduce-scatter.3.cloned.1.call-update) | async-done | bytes 393232 | tf_op jit(solution)/shard_map/reduce_scatter | solution.py:104
  204.3 1.2 fusion.4
  205.5 0.2 fusion.21
  205.7 0.7 broadcast_in_dim.26
  206.4 5.4 %all-to-all-start = ((f32[8,384,8]{1,2,0:T(8,128)}), f32[8,384,8]{1,2,0:T(8,128)S(1)}, u32[]{:S(2)}, u32[]{:S(2)}) async-start(f32[8,384,8]{1,2,0:T(8,128)} %broadcast_in_dim.26), calls=%async_computation.1 | async-start | bytes 196608 | tf_op jit(solution)/shard_map/all_to_all | solution.py:9
  211.8 0.6 fusion.12
  212.4 4.3 all-to-all-done
  216.9 1.3 collective-permute-start.1
  218.2 1.8 collective-permute-done.1
  220.1 0.3 slice.371
  220.4 0.3 slice.365
  220.6 0.3 slice.361
  220.9 0.2 reverse.19
  221.3 0.2 slice.379
  221.5 0.2 slice.375
  221.6 0.2 slice.373
  221.9 0.3 slice.367
  222.2 0.3 slice.363
  222.4 0.3 slice.359
  223.1 0.2 slice.376
  223.3 0.2 slice.374
  226.3 0.2 slice.370
  230.9 0.3 pad.113
  231.3 0.3 pad.128
  231.7 0.3 pad.112
  232.0 0.3 pad.129
  232.3 0.2 add_reduce_fusion
  232.4 0.2 add_reduce_fusion.1
  232.6 0.6 broadcast_in_dim.28
  233.3 9.6 %all-to-all-start.1 = ((f32[32,2,8]{2,1,0:T(2,128)}), f32[32,2,8]{2,1,0:T(2,128)S(1)}, u32[]{:S(2)}, u32[]{:S(2)}) async-start(f32[32,2,8]{2,1,0:T(2,128)} %broadcast_in_dim.28), calls=%async_computation.2 | async-start | bytes 65536 | tf_op jit(solution)/shard_map/all_to_all | solution.py:9
  242.9 0.2 rev.4
  243.2 0.2 rev.5
  243.4 9.3 %all-to-all-done.1 = f32[32,2,8]{2,1,0:T(2,128)S(1)} async-done(((f32[32,2,8]{2,1,0:T(2,128)}), f32[32,2,8]{2,1,0:T(2,128)S(1)}, u32[]{:S(2)}, u32[]{:S(2)}) %all-to-all-start.1) | async-done | bytes 2080 | tf_op jit(solution)/shard_map/all_to_all | solution.py:9
  253.2 0.7 multiply_reduce_fusion
  253.9 0.4 fusion
  254.3 0.2 copy.28
  254.5 0.3 stack.2
  254.8 40.8 %all_to_all.31 = bf16[8,384,512]{1,2,0:T(8,128)(2,1)S(1)} all-to-all(bf16[8,384,512]{1,2,0:T(8,128)(2,1)S(1)} %stack.2), channel_id=1, replica_groups=mesh['batch'=32,'hidden'=8] {'hidden'}, dimensions={0} | all-to-all | bytes 6291456 | tf_op jit(solution)/shard_map/all_to_all | solution.py:128
  295.6 1.6 copy-done.1
  297.2 6.9 %convolution_convert_fusion = bf16[4096,1024]{1,0:T(8,128)(2,1)} fusion(bf16[384,4096]{0,1:T(8,128)(2,1)S(1)} %bitcast.45, f32[384,1024]{1,0:T(8,128)S(1)} %fusion.20), kind=kOutput, calls=%fused_computation | convolution fusion | flops 3227385856 | bytes 13107200 | tf_op jit(solution)/shard_map/dot_general | solution.py:84
  304.2 1.3 broadcast_in_dim.52
  305.4 3.8 all-to-all-start.2
  309.4 9.6 %all-to-all-done.2 = f32[32,1,1]{2,1,0:T(1,128)S(1)} async-done(((f32[32,1,1]{2,1,0:T(1,128)}), f32[32,1,1]{2,1,0:T(1,128)S(1)}, u32[]{:S(2)}, u32[]{:S(2)}) %all-to-all-start.2) | async-done | bytes 160 | tf_op jit(solution)/shard_map/all_to_all | solution.py:9
  319.0 0.9 broadcast_in_dim.53
  319.8 3.9 all-to-all-start.5
  323.7 10.1 %convolution_convert_fusion.2 = bf16[1024,512]{0,1:T(8,128)(2,1)} fusion(bf16[384,512]{1,0:T(8,128)(2,1)S(1)} %copy-done, f32[384,1024]{1,0:T(8,128)S(1)} %fusion.20, bf16[384,4096]{0,1:T(8,128)(2,1)} %bitcast.46, bf16[1024,4096]{1,0:T(8,128)(2,1)} %all-gather.5.cloned.1.call-done), kind=kOutput, calls=%fused_computation.6 | convolution fusion | flops 3627941888 | bytes 14548992 | tf_op jit(solution)/shard_map/dot_general | solution.py:84
  333.8 8.2 %all-to-all-done.5 = f32[32,512,8]{1,2,0:T(8,128)S(1)} async-done(((f32[32,512,8]{1,2,0:T(8,128)}), f32[32,512,8]{1,2,0:T(8,128)S(1)}, u32[]{:S(2)}, u32[]{:S(2)}) %all-to-all-start.5) | async-done | bytes 524320 | tf_op jit(solution)/shard_map/all_to_all | solution.py:9
  342.0 4.0 all-to-all-start.4
  346.0 0.6 reduce_sum.47
  347.3 0.7 reduce_sum.49
  348.0 29.1 %all-to-all-done.4 = bf16[32,16,1024]{2,1,0:T(8,128)(2,1)S(1)} async-done(((bf16[32,16,1024]{2,1,0:T(8,128)(2,1)}), bf16[32,16,1024]{2,1,0:T(8,128)(2,1)S(1)}, u32[]{:S(2)}, u32[]{:S(2)}) %all-to-all-start.4) | async-done | bytes 1048608 | tf_op jit(solution)/shard_map/all_to_all | solution.py:70
  377.1 0.8 convert_reduce_fusion
  377.9 57.8 %reduce-scatter.5.cloned.1.call-done = bf16[128,1024]{1,0:T(8,128)(2,1)} async-done(((bf16[4096,1024]{1,0:T(8,128)(2,1)}), bf16[128,1024]{1,0:T(8,128)(2,1)}) %reduce-scatter.5.cloned.1.call-update) | async-done | bytes 262160 | tf_op jit(solution)/shard_map/reduce_scatter | solution.py:141
  435.7 1.0 convert_bitcast_fusion
  436.7 1.0 copy.29
  (172 shorter events, 9.1 us)
Async XLA Ops:
  7.2 58.3 %copy-start = (bf16[384,512]{1,0:T(8,128)(2,1)S(1)}, bf16[384,512]{1,0:T(8,128)(2,1)}, u32[]{:S(2)}) copy-start(bf16[384,512]{1,0:T(8,128)(2,1)} %param.8) | copy-start | bytes 1179652
  7.2 58.3 %all-gather.3.cloned.1.call-start = ((), (), s32[]{:S(2)}) async-start(), calls=%async_computation.8 | async-start | bytes 1081344 | tf_op jit(solution)/shard_map/all_gather | solution.py:95
  7.9 141.8 %all-gather.5.cloned.1.call-start = ((), (), s32[]{:S(2)}) async-start(), calls=%async_computation.9 | async-start | bytes 8650752 | tf_op jit(solution)/shard_map/all_gather | solution.py:101
  8.7 195.6 %reduce-scatter.3.cloned.1.call-start = ((), (), s32[]{:S(2)}) async-start(), calls=%async_computation.10 | async-start | bytes 3538944 | tf_op jit(solution)/shard_map/reduce_scatter | solution.py:104
  157.9 0.7 copy-start.6
  157.9 3.2 copy-start.7
  157.9 3.2 copy-start.8
  157.9 47.6 %copy-start.5 = (bf16[512,8]{0,1:T(8,128)(2,1)S(1)}, bf16[512,8]{0,1:T(8,128)(2,1)}, u32[]{:S(2)}) copy-start(bf16[512,8]{0,1:T(8,128)(2,1)} %param.11) | copy-start | bytes 24580
  158.5 61.4 %copy-start.4 = (f32[8,384]{1,0:T(8,128)S(1)}, f32[8,384]{1,0:T(8,128)}, u32[]{:S(2)}) copy-start(f32[8,384]{1,0:T(8,128)} %param.12) | copy-start | bytes 36868
  159.7 52.1 %collective-permute-start = (s32[1]{0:T(128)}, s32[1]{0:T(128)}, u32[]{:S(2)}, u32[]{:S(2)}) collective-permute-start(s32[1]{0:T(128)} %add.218), channel_id=1, source_target_pairs={{8,0},{16,8},{24,16},{32,24},{40,32},{48,40},{56,48},{64,56},{72,6... | collective-permute-start | bytes 20 | tf_op jit(solution)/shard_map/ppermute | solution.py:21
  205.7 48.1 %copy-start.2 = (bf16[384,512]{1,0:T(8,128)(2,1)S(1)}, bf16[384,512]{1,0:T(8,128)(2,1)}, u32[]{:S(2)}) copy-start(bf16[384,512]{1,0:T(8,128)(2,1)} %reduce-scatter.3.cloned.1.call-done) | copy-start | bytes 1179652
  206.4 10.4 %all-to-all-start = ((f32[8,384,8]{1,2,0:T(8,128)}), f32[8,384,8]{1,2,0:T(8,128)S(1)}, u32[]{:S(2)}, u32[]{:S(2)}) async-start(f32[8,384,8]{1,2,0:T(8,128)} %broadcast_in_dim.26), calls=%async_computation.1 | async-start | bytes 196608 | tf_op jit(solution)/shard_map/all_to_all | solution.py:9
  216.9 3.1 collective-permute-start.1
  233.3 19.4 %all-to-all-start.1 = ((f32[32,2,8]{2,1,0:T(2,128)}), f32[32,2,8]{2,1,0:T(2,128)S(1)}, u32[]{:S(2)}, u32[]{:S(2)}) async-start(f32[32,2,8]{2,1,0:T(2,128)} %broadcast_in_dim.28), calls=%async_computation.2 | async-start | bytes 65536 | tf_op jit(solution)/shard_map/all_to_all | solution.py:9
  242.8 192.9 %reduce-scatter.5.cloned.1.call-start = ((), (), s32[]{:S(2)}) async-start(), calls=%async_computation.11 | async-start | bytes 8650752 | tf_op jit(solution)/shard_map/reduce_scatter | solution.py:141
  253.8 55.4 %copy-start.3 = (f32[8,384]{1,0:T(8,128)}, f32[8,384]{1,0:T(8,128)S(1)}, u32[]{:S(2)}) copy-start(f32[8,384]{1,0:T(8,128)S(1)} %get-tuple-element.31) | copy-start | bytes 36868
  295.6 1.6 copy-start.1
  305.4 13.6 %all-to-all-start.2 = ((f32[32,1,1]{2,1,0:T(1,128)}), f32[32,1,1]{2,1,0:T(1,128)S(1)}, u32[]{:S(2)}, u32[]{:S(2)}) async-start(f32[32,1,1]{2,1,0:T(1,128)} %broadcast_in_dim.52), calls=%async_computation.3 | async-start | bytes 32768 | tf_op jit(solution)/shard_map/all_to_all | solution.py:9
  319.8 22.2 %all-to-all-start.5 = ((f32[32,512,8]{1,2,0:T(8,128)}), f32[32,512,8]{1,2,0:T(8,128)S(1)}, u32[]{:S(2)}, u32[]{:S(2)}) async-start(f32[32,512,8]{1,2,0:T(8,128)} %broadcast_in_dim.53), calls=%async_computation.7 | async-start | bytes 1048576 | tf_op jit(solution)/shard_map/all_to_all | solution.py:9
  342.0 35.1 %all-to-all-start.4 = ((bf16[32,16,1024]{2,1,0:T(8,128)(2,1)}), bf16[32,16,1024]{2,1,0:T(8,128)(2,1)S(1)}, u32[]{:S(2)}, u32[]{:S(2)}) async-start(bf16[32,16,1024]{2,1,0:T(8,128)(2,1)} %bitcast.47), calls=%async_computation.5 | async-start | bytes 2097152 | tf_op jit(solution)/shard_map/all_to_all | solution.py:70
Sparse Core Ops, SparseCore 0:
  10.5 54.8 all-gather.2
  67.9 81.7 all-gather.4
  158.0 46.1 reduce-scatter.2
  304.3 131.4 reduce-scatter.4
